TPU v7x, 32 devices: a whole 2x2x4 slice. The times are simulated.
32 devices in a mesh: pb: 4 (over x, core), pq: 8 (over z, y).
Axes of the slice: x: 2, y: 2, z: 4, core: 2. Of those that a mesh axis runs over, the one named last changes fastest.
Arguments:
- chol_vv: bfloat16 [176, 1792, 1792], P('pb', 'pq'), may hold values from -6 to 6
- chol_ov: bfloat16 [176, 256, 1792], P('pb', 'pq'), may hold values from -6 to 6
- chol_oo: bfloat16 [176, 256, 256], P('pb', 'pq'), may hold values from -6 to 6
- chol_vo: bfloat16 [176, 256, 1792], P('pb', None, 'pq'), may hold values from -6 to 6
- amplitudes: bfloat16 [256, 1792], P(None, 'pq'), may hold values from -0.125 to 0.125
Outputs:
- dressed: bfloat16 [176, 256, 1792], P('pb', 'pq')
- fock_ov: float32 [256, 1792], P('pq')
All inputs are finite; a program needn't handle non-finite values.
Results may differ from a plain program's by a relative error of at most 0.0081.
Values may be sent and summed in bfloat16 or wider, within the bound.
A program may use at most 128 MiB of HBM per device.

v0:
```python
import jax
import jax.numpy as jnp
from jax import lax
from jax.sharding import PartitionSpec as P


def per_device(chol_vv, chol_ov, chol_oo, chol_vo, amplitudes):
    batch = chol_vv.shape[0]
    occ_rows = chol_ov.shape[1]
    whole_amps = lax.all_gather(amplitudes, "pq", axis=1, tiled=True)
    lprime = (
        chol_oo.astype(jnp.float32)
        + jnp.einsum("qjb,ib->qji", chol_ov, whole_amps, preferred_element_type=jnp.float32)
    ).astype(jnp.bfloat16)
    direct = jnp.einsum("qab,ib->qia", chol_vv, whole_amps, preferred_element_type=jnp.float32)
    partial_sum = chol_vo.astype(jnp.float32) + direct
    occupied = jnp.einsum(
        "qji,ja->qia",
        lax.all_gather(lprime, "pq", axis=1, tiled=True),
        amplitudes,
        preferred_element_type=jnp.float32,
    )
    local_dressed = (partial_sum - occupied).astype(jnp.bfloat16)
    dressed = lax.all_to_all(local_dressed, "pq", split_axis=1, concat_axis=2, tiled=True)
    row_start = lax.axis_index("pq") * occ_rows
    own_amps = lax.dynamic_slice_in_dim(whole_amps, row_start, occ_rows, 0)
    local_coulomb = 2.0 * jnp.einsum(
        "qia,ia->q", dressed, own_amps, preferred_element_type=jnp.float32
    )
    coulomb = lax.psum(local_coulomb, "pq")
    local_fock = jnp.sum(coulomb[:, None, None] * dressed.astype(jnp.float32), axis=0)
    fock_ov = lax.psum(local_fock, "pb") / (batch * lax.axis_size("pb"))
    return (dressed, fock_ov)


def solution(mesh):
    in_specs = (
        P("pb", "pq", None),
        P("pb", "pq", None),
        P("pb", "pq", None),
        P("pb", None, "pq"),
        P(None, "pq"),
    )
    out_specs = (P("pb", "pq", None), P("pq", None))
    return jax.shard_map(
        per_device, mesh=mesh, in_specs=in_specs, out_specs=out_specs, check_vma=False
    )
```

profile of v0, /device:TPU:0, one launch (start us, length us, event | category | flops | bytes accessed | tf_op | source)
XLA Modules:
  0.0 394.0 jit_solution(11344486963419450905)
XLA Ops:
  7.2 0.0 all-gather.2.cloned.1.call-start
  7.2 34.5 %all_gather.6 = bf16[256,1792]{0,1:T(8,128)(2,1)S(1)} all-gather(bf16[256,224]{0,1:T(8,128)(2,1)} %param.9), channel_id=1, replica_groups=mesh['pb'=4,'pq'=8] {'pq'}, dimensions={1}, use_global_device_ids=true | all-gather | bytes 1032192 | tf_op jit(solution)/shard_map/all_gather | solution.py:10
  41.7 5.0 %add_convert_fusion = bf16[44,32,256]{2,1,0:T(8,128)(2,1)} fusion(bf16[44,32,256]{2,1,0:T(8,128)(2,1)} %param.7, bf16[44,32,1792]{2,1,0:T(8,128)(2,1)} %param.6, bf16[256,1792]{0,1:T(8,128)(2,1)S(1)} %all_gather.6), kind=kOutput, calls=%fused_computation.6 | convolution fusion | flops 1292926976 | bytes 7405568 | tf_op jit(solution)/shard_map/qjb,ib->qji/dot_general | solution.py:13
  46.6 0.0 all-gather.2.cloned.1.call-update
  46.6 0.0 copy-start
  46.7 19.8 %fusion.11 = f32[256,44,224]{0,2,1:T(8,128)} fusion(bf16[44,224,1792]{2,1,0:T(8,128)(2,1)} %param.5, bf16[256,1792]{0,1:T(8,128)(2,1)S(1)} %all_gather.6), kind=kOutput, calls=%fused_computation.10 | convolution fusion | flops 9042919424 | bytes 46333952 | tf_op jit(solution)/shard_map/qab,ib->qia/dot_general | solution.py:15
  66.4 73.5 %all-gather.2.cloned.1.call-done = bf16[44,256,256]{2,1,0:T(8,128)(2,1)} async-done(((bf16[44,32,256]{2,1,0:T(8,128)(2,1)}), bf16[44,256,256]{2,1,0:T(8,128)(2,1)}) %all-gather.2.cloned.1.call-update) | async-done | bytes 5767184 | tf_op jit(solution)/shard_map/all_gather | solution.py:19
  139.9 0.0 copy-done
  139.9 10.7 %fusion.1 = bf16[44,256,224]{1,2,0:T(8,128)(2,1)} fusion(f32[256,44,224]{0,2,1:T(8,128)} %fusion.11, bf16[44,256,224]{1,2,0:T(8,128)(2,1)} %param.8, bf16[44,256,256]{2,1,0:T(8,128)(2,1)} %all-gather.2.cloned.1.call-done, bf16[256,224]{0,1:T(8,128)(2,1)S(1)} %copy-done), kind=kOutput, calls=%fused_computation.3 | convolution fusion | flops 1301938176 | bytes 26066944 | tf_op jit(solution)/shard_map/qji,ja->qia/dot_general | solution.py:17
  150.6 8.8 %copy.14 = bf16[44,256,224]{2,0,1:T(8,128)(2,1)} copy(bf16[44,256,224]{1,2,0:T(8,128)(2,1)} %fusion.1) | data formatting | bytes 10092544 | tf_op jit(solution)/shard_map/convert_element_type | solution.py:23
  159.5 4.7 %all-to-all-start = ((bf16[44,256,224]{2,0,1:T(8,128)(2,1)}), bf16[44,256,224]{2,0,1:T(8,128)(2,1)}, u32[]{:S(2)}, u32[]{:S(2)}) async-start(bf16[44,256,224]{2,0,1:T(8,128)(2,1)} %copy.14), calls=%async_computation | async-start | bytes 12582912 | tf_op jit(solution)/shard_map/all_to_all | solution.py:24
  164.2 0.2 all-reduce.2.cloned.1.call-start
  164.5 0.2 dynamic-slice_bitcast_fusion
  164.7 0.3 copy.19
  165.0 136.1 %all-to-all-done = bf16[44,256,224]{2,0,1:T(8,128)(2,1)} async-done(((bf16[44,256,224]{2,0,1:T(8,128)(2,1)}), bf16[44,256,224]{2,0,1:T(8,128)(2,1)}, u32[]{:S(2)}, u32[]{:S(2)}) %all-to-all-start) | async-done | bytes 5046304 | tf_op jit(solution)/shard_map/all_to_all | solution.py:24
  301.1 8.6 %copy.16 = bf16[44,32,8,224]{3,2,1,0:T(8,128)(2,1)} copy(bf16[44,32,8,224]{3,0,1,2:T(8,128)(2,1)} %bitcast.5) | data formatting | bytes 10092544 | tf_op jit(solution)/shard_map/all_to_all | solution.py:24
  309.7 11.0 %all_to_all.16 = bf16[44,32,1792]{2,1,0:T(8,128)(2,1)} reshape(bf16[44,32,8,224]{3,2,1,0:T(8,128)(2,1)} %copy.16) | data formatting | bytes 10092544 | tf_op jit(solution)/shard_map/all_to_all | solution.py:24
  320.7 7.9 %fusion.7 = f32[44]{0:T(128)S(1)} fusion(bf16[32,1792,1]{1,2,0:T(2,128)(2,1)S(1)} %copy.19, bf16[44,32,1792]{2,1,0:T(8,128)(2,1)} %all_to_all.16), kind=kOutput, calls=%fused_computation.8 | convolution fusion | flops 5046316 | bytes 5161136 | tf_op jit(solution)/shard_map/qia,ia->q/dot_general | solution.py:27
  328.5 19.7 %psum.14 = f32[44]{0:T(128)S(1)} all-reduce(f32[44]{0:T(128)S(1)} %fusion.7), channel_id=1, replica_groups=mesh['pb'=4,'pq'=8] {'pq'}, use_global_device_ids=true, to_apply=%region_0.0 | all-reduce | flops 44 | bytes 352 | tf_op jit(solution)/shard_map/psum | solution.py:30
  348.2 4.8 %copy.15 = bf16[44,256,224]{2,1,0:T(8,128)(2,1)S(1)} copy(bf16[44,256,224]{2,0,1:T(8,128)(2,1)} %all-to-all-done) | data formatting | bytes 10092544 | tf_op jit(solution)/shard_map/all_to_all | solution.py:24
  353.0 1.9 multiply_reduce_fusion
  354.9 0.2 copy.17
  355.0 0.8 reduce_sum.12
  355.9 0.0 all-reduce.2.cloned.1.call-update
  355.9 29.6 %all-reduce.2.cloned.1.call-done = f32[32,1792]{1,0:T(8,128)} async-done(((f32[32,1792]{1,0:T(8,128)}), f32[32,1792]{1,0:T(8,128)}) %all-reduce.2.cloned.1.call-update) | async-done | bytes 229392 | tf_op jit(solution)/shard_map/psum | solution.py:32
  385.5 1.6 broadcast_multiply_fusion
Async XLA Ops:
  7.2 132.8 %all-gather.2.cloned.1.call-start = ((), (), s32[]{:S(2)}) async-start(), calls=%async_computation.1 | async-start | bytes 6488064 | tf_op jit(solution)/shard_map/all_gather | solution.py:19
  46.6 93.3 %copy-start = (bf16[256,224]{0,1:T(8,128)(2,1)S(1)}, bf16[256,224]{0,1:T(8,128)(2,1)}, u32[]{:S(2)}) copy-start(bf16[256,224]{0,1:T(8,128)(2,1)} %param.9) | copy-start | bytes 344068
  159.5 141.6 %all-to-all-start = ((bf16[44,256,224]{2,0,1:T(8,128)(2,1)}), bf16[44,256,224]{2,0,1:T(8,128)(2,1)}, u32[]{:S(2)}, u32[]{:S(2)}) async-start(bf16[44,256,224]{2,0,1:T(8,128)(2,1)} %copy.14), calls=%async_computation | async-start | bytes 12582912 | tf_op jit(solution)/shard_map/all_to_all | solution.py:24
  164.2 221.2 %all-reduce.2.cloned.1.call-start = ((), (), s32[]{:S(2)}) async-start(), calls=%async_computation.2 | async-start | bytes 458752 | tf_op jit(solution)/shard_map/psum | solution.py:32
Sparse Core Ops, SparseCore 0:
  46.8 93.1 all-gather.1
  356.0 29.4 all-reduce.1
where the time goes:
time: 395 us; the launch traced here: 394 us
  waiting for transfers between devices  239 us (61%)
  blocking collectives  54.1 us (14%)
  matrix products  43.3 us (11%)
  local copies, waits for them, and re-layouts  34.7 us (9%)
  between operations  14.1 us (4%)
  starting transfers between devices  5.01 us (1%)
    all_to_all x1, waiting for transfers between devices, per_device(): lax.all_to_all(local_dressed, 'pq', split_axis=1, concat_axis=2, tiled=True)  136 us
    all_gather x1, waiting for transfers between devices, per_device(): lax.all_gather(lprime, 'pq', axis=1, tiled=True)  73.5 us
    all_gather x1, blocking collectives, per_device(): whole_amps = lax.all_gather(amplitudes, 'pq', axis=1, tiled=True)  34.5 us
    psum x1, waiting for transfers between devices, per_device(): fock_ov = lax.psum(local_fock, 'pb') / (batch * lax.axis_size('pb'))  29.6 us
    all_to_all x3, local copies, waits for them, and re-layouts, per_device(): lax.all_to_all(local_dressed, 'pq', split_axis=1, concat_axis=2, tiled=True)  24.4 us
    dot_general x1, matrix products, per_device(): jnp.einsum('qab,ib->qia', chol_vv, whole_amps, preferred_element_type=jnp...  19.8 us
    psum x1, blocking collectives, per_device(): coulomb = lax.psum(local_coulomb, 'pq')  19.7 us
    dot_general x1, matrix products, per_device(): jnp.einsum('qji,ja->qia', lax.all_gather(lprime, 'pq', axis=1, tiled=True...  10.7 us
  transfers between devices with their start and end apart: 3, of which 3 were waited for; matrix products, arithmetic and copies ran while one was open for 5% of the time, Pallas kernels for 0%

commit v1 on v0

--- a/solution.py
+++ b/solution.py
@@ -29,7 +29,7 @@
     )
     coulomb = lax.psum(local_coulomb, "pq")
     local_fock = jnp.sum(coulomb[:, None, None] * dressed.astype(jnp.float32), axis=0)
-    fock_ov = lax.psum(local_fock, "pb") / (batch * lax.axis_size("pb"))
+    fock_ov = jnp.sum(lax.all_gather(local_fock, "pb"), axis=0) / (batch * lax.axis_size("pb"))
     return (dressed, fock_ov)
 
 

time: 395 us -> 373 us (0.944)
  waiting for transfers between devices: 239 us -> 210 us
  blocking collectives: 54.1 us -> 63.4 us
    psum x1 -> x0, waiting for transfers between devices: 29.6 us -> none  [per_device(): fock_ov = lax.psum(local_fock, 'pb') / (batch * lax.axis_size('pb'))]
    all_gather x0 -> x1, blocking collectives: none -> 9.29 us  [per_device(): lax.all_gather(local_fock, 'pb')]
  transfers between devices with their start and end apart: 3 -> 2, of which waited for: 3 -> 2; matrix products, arithmetic and copies ran while one was open for 5% -> 5% of each run, Pallas kernels for 0% -> 0%
where the time goes in v1:
time: 373 us; the launch traced here: 372 us
  waiting for transfers between devices  210 us (56%)
  blocking collectives  63.4 us (17%)
  matrix products  43.3 us (12%)
  local copies, waits for them, and re-layouts  33.9 us (9%)
  between operations  14.1 us (4%)
  starting transfers between devices  4.96 us (1%)
    all_to_all x1, waiting for transfers between devices, per_device(): lax.all_to_all(local_dressed, 'pq', split_axis=1, concat_axis=2, tiled=True)  136 us
    all_gather x1, waiting for transfers between devices, per_device(): lax.all_gather(lprime, 'pq', axis=1, tiled=True)  73.5 us
    all_gather x1, blocking collectives, per_device(): whole_amps = lax.all_gather(amplitudes, 'pq', axis=1, tiled=True)  34.5 us
    all_to_all x3, local copies, waits for them, and re-layouts, per_device(): lax.all_to_all(local_dressed, 'pq', split_axis=1, concat_axis=2, tiled=True)  24.4 us
    dot_general x1, matrix products, per_device(): jnp.einsum('qab,ib->qia', chol_vv, whole_amps, preferred_element_type=jnp...  19.8 us
    psum x1, blocking collectives, per_device(): coulomb = lax.psum(local_coulomb, 'pq')  19.7 us
    dot_general x1, matrix products, per_device(): jnp.einsum('qji,ja->qia', lax.all_gather(lprime, 'pq', axis=1, tiled=True...  10.7 us
    all_gather x1, blocking collectives, per_device(): lax.all_gather(local_fock, 'pb')  9.29 us
  transfers between devices with their start and end apart: 2, of which 2 were waited for; matrix products, arithmetic and copies ran while one was open for 5% of the time, Pallas kernels for 0%

profile of v1, /device:TPU:0, one launch (start us, length us, event | category | flops | bytes accessed | tf_op | source)
XLA Modules:
  0.0 372.0 jit_solution(1380634320363192755)
XLA Ops:
  7.2 0.0 all-gather.2.cloned.1.call-start
  7.2 34.5 %all_gather.12 = bf16[256,1792]{0,1:T(8,128)(2,1)S(1)} all-gather(bf16[256,224]{0,1:T(8,128)(2,1)} %param.9), channel_id=1, replica_groups=mesh['pb'=4,'pq'=8] {'pq'}, dimensions={1}, use_global_device_ids=true | all-gather | bytes 1032192 | tf_op jit(solution)/shard_map/all_gather | solution.py:10
  41.7 5.0 %add_convert_fusion = bf16[44,32,256]{2,1,0:T(8,128)(2,1)} fusion(bf16[44,32,256]{2,1,0:T(8,128)(2,1)} %param.7, bf16[44,32,1792]{2,1,0:T(8,128)(2,1)} %param.6, bf16[256,1792]{0,1:T(8,128)(2,1)S(1)} %all_gather.12), kind=kOutput, calls=%fused_computation.6 | convolution fusion | flops 1292926976 | bytes 7405568 | tf_op jit(solution)/shard_map/qjb,ib->qji/dot_general | solution.py:13
  46.6 0.0 all-gather.2.cloned.1.call-update
  46.6 0.0 copy-start
  46.7 19.8 %fusion.11 = f32[256,44,224]{0,2,1:T(8,128)} fusion(bf16[44,224,1792]{2,1,0:T(8,128)(2,1)} %param.5, bf16[256,1792]{0,1:T(8,128)(2,1)S(1)} %all_gather.12), kind=kOutput, calls=%fused_computation.10 | convolution fusion | flops 9042919424 | bytes 46333952 | tf_op jit(solution)/shard_map/qab,ib->qia/dot_general | solution.py:15
  66.4 73.5 %all-gather.2.cloned.1.call-done = bf16[44,256,256]{2,1,0:T(8,128)(2,1)} async-done(((bf16[44,32,256]{2,1,0:T(8,128)(2,1)}), bf16[44,256,256]{2,1,0:T(8,128)(2,1)}) %all-gather.2.cloned.1.call-update) | async-done | bytes 5767184 | tf_op jit(solution)/shard_map/all_gather | solution.py:19
  139.9 0.0 copy-done
  139.9 10.7 %fusion.1 = bf16[44,256,224]{1,2,0:T(8,128)(2,1)} fusion(f32[256,44,224]{0,2,1:T(8,128)} %fusion.11, bf16[44,256,224]{1,2,0:T(8,128)(2,1)} %param.8, bf16[44,256,256]{2,1,0:T(8,128)(2,1)} %all-gather.2.cloned.1.call-done, bf16[256,224]{0,1:T(8,128)(2,1)S(1)} %copy-done), kind=kOutput, calls=%fused_computation.3 | convolution fusion | flops 1301938176 | bytes 26066944 | tf_op jit(solution)/shard_map/qji,ja->qia/dot_general | solution.py:17
  150.6 8.7 %copy.14 = bf16[44,256,224]{2,0,1:T(8,128)(2,1)} copy(bf16[44,256,224]{1,2,0:T(8,128)(2,1)} %fusion.1) | data formatting | bytes 10092544 | tf_op jit(solution)/shard_map/convert_element_type | solution.py:23
  159.4 4.9 %all-to-all-start = ((bf16[44,256,224]{2,0,1:T(8,128)(2,1)}), bf16[44,256,224]{2,0,1:T(8,128)(2,1)}, u32[]{:S(2)}, u32[]{:S(2)}) async-start(bf16[44,256,224]{2,0,1:T(8,128)(2,1)} %copy.14), calls=%async_computation | async-start | bytes 12582912 | tf_op jit(solution)/shard_map/all_to_all | solution.py:24
  164.3 0.2 dynamic-slice_bitcast_fusion
  164.5 0.3 copy.19
  164.8 136.2 %all-to-all-done = bf16[44,256,224]{2,0,1:T(8,128)(2,1)} async-done(((bf16[44,256,224]{2,0,1:T(8,128)(2,1)}), bf16[44,256,224]{2,0,1:T(8,128)(2,1)}, u32[]{:S(2)}, u32[]{:S(2)}) %all-to-all-start) | async-done | bytes 5046304 | tf_op jit(solution)/shard_map/all_to_all | solution.py:24
  301.0 8.6 %copy.16 = bf16[44,32,8,224]{3,2,1,0:T(8,128)(2,1)} copy(bf16[44,32,8,224]{3,0,1,2:T(8,128)(2,1)} %bitcast.5) | data formatting | bytes 10092544 | tf_op jit(solution)/shard_map/all_to_all | solution.py:24
  309.6 11.0 %all_to_all.16 = bf16[44,32,1792]{2,1,0:T(8,128)(2,1)} reshape(bf16[44,32,8,224]{3,2,1,0:T(8,128)(2,1)} %copy.16) | data formatting | bytes 10092544 | tf_op jit(solution)/shard_map/all_to_all | solution.py:24
  320.5 7.9 %fusion.7 = f32[44]{0:T(128)S(1)} fusion(bf16[32,1792,1]{1,2,0:T(2,128)(2,1)S(1)} %copy.19, bf16[44,32,1792]{2,1,0:T(8,128)(2,1)} %all_to_all.16), kind=kOutput, calls=%fused_computation.8 | convolution fusion | flops 5046316 | bytes 5161136 | tf_op jit(solution)/shard_map/qia,ia->q/dot_general | solution.py:27
  328.4 19.7 %psum.7 = f32[44]{0:T(128)S(1)} all-reduce(f32[44]{0:T(128)S(1)} %fusion.7), channel_id=1, replica_groups=mesh['pb'=4,'pq'=8] {'pq'}, use_global_device_ids=true, to_apply=%region_0.0 | all-reduce | flops 44 | bytes 352 | tf_op jit(solution)/shard_map/psum | solution.py:30
  348.1 4.8 %copy.15 = bf16[44,256,224]{2,1,0:T(8,128)(2,1)S(1)} copy(bf16[44,256,224]{2,0,1:T(8,128)(2,1)} %all-to-all-done) | data formatting | bytes 10092544 | tf_op jit(solution)/shard_map/all_to_all | solution.py:24
  352.9 1.9 multiply_reduce_fusion
  354.8 0.2 copy.17
  354.9 0.1 all_gather.14
  355.1 9.3 %all_gather.15 = f32[4,32,1792]{2,1,0:T(8,128)S(1)} all-gather(f32[1,32,1792]{2,1,0:T(8,128)S(1)} %all_gather.14), channel_id=1, replica_groups=mesh['pb'=4,'pq'=8] {'pb'}, dimensions={0}, use_global_device_ids=true | all-gather | bytes 1146880 | tf_op jit(solution)/shard_map/all_gather | solution.py:32
  364.4 0.1 reduce_sum.19
  364.4 0.7 broadcast_multiply_fusion
Async XLA Ops:
  7.2 132.8 %all-gather.2.cloned.1.call-start = ((), (), s32[]{:S(2)}) async-start(), calls=%async_computation.1 | async-start | bytes 6488064 | tf_op jit(solution)/shard_map/all_gather | solution.py:19
  46.6 93.3 %copy-start = (bf16[256,224]{0,1:T(8,128)(2,1)S(1)}, bf16[256,224]{0,1:T(8,128)(2,1)}, u32[]{:S(2)}) copy-start(bf16[256,224]{0,1:T(8,128)(2,1)} %param.9) | copy-start | bytes 344068
  159.4 141.6 %all-to-all-start = ((bf16[44,256,224]{2,0,1:T(8,128)(2,1)}), bf16[44,256,224]{2,0,1:T(8,128)(2,1)}, u32[]{:S(2)}, u32[]{:S(2)}) async-start(bf16[44,256,224]{2,0,1:T(8,128)(2,1)} %copy.14), calls=%async_computation | async-start | bytes 12582912 | tf_op jit(solution)/shard_map/all_to_all | solution.py:24
Sparse Core Ops, SparseCore 0:
  46.8 93.1 all-gather.1
